TPU v7x, 32 devices: a whole 2x2x4 slice. The times are simulated.
32 devices in a mesh: seq: 2 (over x), tensor: 4 (over z), bucket: 4 (over y, core).
Axes of the slice: x: 2, y: 2, z: 4, core: 2. Of those that a mesh axis runs over, the one named last changes fastest.
Arguments:
- queries: bfloat16 [4, 1024, 3072], P('bucket', ('seq', 'tensor')), may hold values from -6 to 6
- keys: bfloat16 [4, 1024, 3072], P('bucket', ('seq', 'tensor')), may hold values from -6 to 6
- values: bfloat16 [4, 1024, 3072], P('bucket', ('seq', 'tensor')), may hold values from -6 to 6
- lengths: int32 [4], P('bucket'), may hold values from 256 to 1024, as said below
- out_weight: bfloat16 [3072, 3072], P(('seq', 'bucket'), 'tensor'), may hold values from -0.109375 to 0.109375
Outputs:
- projected: bfloat16 [4, 1024, 3072], P('bucket', ('seq', 'tensor'))
Inputs may be any that keep to these rules, and one draw needn't show every extreme that they name: `lengths`: each bucket has 256 to 1024 live tokens, and at least one bucket has all 1024.
All inputs are finite; a program needn't handle non-finite values.
Results may differ from a plain program's by a relative error of at most 0.018.
Values may be sent and summed in bfloat16 or wider, within the bound.
No kernel may reach another device: no remote copies, remote signals or barrier semaphores. Data moves between devices by JAX's collectives and lax.ppermute only.
A program may use at most 128 MiB of HBM per device.

v0:
```python
import jax
import jax.numpy as jnp
from jax import lax
from jax.sharding import PartitionSpec as P

HS = 128
MASKED_SCORE = -1e30


def shards(queries, keys, values, lengths, out_weight):
    tok_rows = queries.shape[1]
    n_tensor = lax.axis_size("tensor")
    tensor_index = lax.axis_index("tensor")
    live_len = lengths[0]
    local_q, local_k, local_v = (
        lax.all_to_all(queries[0], "seq", split_axis=1, concat_axis=0, tiled=True),
        lax.all_to_all(keys[0], "seq", split_axis=1, concat_axis=0, tiled=True),
        lax.all_to_all(values[0], "seq", split_axis=1, concat_axis=0, tiled=True),
    )
    row_count, col_count = local_q.shape
    head_count = col_count // HS
    query_heads = local_q.reshape(row_count, head_count, HS)

    def spots(first_row, total_rows):
        index_row = first_row + jnp.arange(total_rows, dtype=jnp.int32)
        owner = index_row // row_count
        within = index_row % row_count
        return (within // tok_rows * n_tensor + owner) * tok_rows + within % tok_rows

    query_usable = spots(tensor_index * row_count, row_count) < live_len
    initial = (
        jnp.full((row_count, head_count), MASKED_SCORE, jnp.float32),
        jnp.zeros((row_count, head_count), jnp.float32),
        jnp.zeros((row_count, head_count, HS), jnp.float32),
    )
    carried = initial
    first_row = jnp.int32(0)
    key_rows = lax.all_gather(local_k, "tensor", axis=0, tiled=True)
    value_rows = lax.all_gather(local_v, "tensor", axis=0, tiled=True)
    for offset in range(key_rows.shape[0] // row_count):
        row_peak, row_sum, accumulated = carried
        key_tile = key_rows[offset * row_count : (offset + 1) * row_count].reshape(
            row_count, head_count, HS
        )
        value_tile = value_rows[offset * row_count : (offset + 1) * row_count].reshape(
            row_count, head_count, HS
        )
        key_usable = spots(first_row + offset * row_count, row_count) < live_len
        scores = jnp.einsum(
            "qhd,khd->qhk", query_heads, key_tile, preferred_element_type=jnp.float32
        ) * HS ** (-0.5)
        scores = jnp.where(key_usable[None, None, :], scores, MASKED_SCORE)
        peak_new = jnp.maximum(row_peak, jnp.max(scores, axis=-1))
        exponent = jnp.where(key_usable[None, None, :], jnp.exp(scores - peak_new[..., None]), 0.0)
        rescale = jnp.exp(row_peak - peak_new)
        accumulated = accumulated * rescale[..., None] + jnp.einsum(
            "qhk,khd->qhd",
            exponent.astype(jnp.bfloat16),
            value_tile,
            preferred_element_type=jnp.float32,
        )
        carried = (peak_new, row_sum * rescale + jnp.sum(exponent, axis=-1), accumulated)
    row_peak, row_sum, accumulated = carried
    attended = accumulated / row_sum[..., None]
    mixed = jnp.where(query_usable[:, None], attended.reshape(row_count, col_count), 0.0).astype(
        jnp.bfloat16
    )
    restored = lax.all_to_all(mixed, "seq", split_axis=0, concat_axis=1, tiled=True)
    wide_weight = lax.all_gather(out_weight, "tensor", axis=1, tiled=True)
    summed = jnp.dot(
        restored,
        lax.all_gather(wide_weight, ("seq", "bucket"), axis=0, tiled=True),
        preferred_element_type=jnp.float32,
    )
    return summed.astype(jnp.bfloat16)[None]


def solution(mesh):
    in_specs = (
        P("bucket", ("seq", "tensor"), None),
        P("bucket", ("seq", "tensor"), None),
        P("bucket", ("seq", "tensor"), None),
        P("bucket"),
        P(("seq", "bucket"), "tensor"),
    )
    out_specs = P("bucket", ("seq", "tensor"), None)
    return jax.shard_map(shards, mesh=mesh, in_specs=in_specs, out_specs=out_specs, check_vma=False)
```

profile of v0, /device:TPU:0, one launch (start us, length us, event | category | flops | bytes accessed | tf_op | source)
XLA Modules:
  0.0 309.9 jit_solution(5005568359367810147)
XLA Ops:
  7.3 1.5 copy.68
  8.8 14.8 %all_to_all.70 = bf16[128,2,1536]{0,2,1:T(8,128)(2,1)S(1)} all-to-all(bf16[128,2,1536]{0,2,1:T(8,128)(2,1)S(1)} %bitcast.125), channel_id=1, replica_groups=mesh['seq'=2,'tensor'=4,'bucket'=4] {'seq'}, dimensions={1} | all-to-all | bytes 1572864 | tf_op jit(solution)/shard_map/all_to_all | solution.py:17
  25.3 12.5 %all_to_all.71 = bf16[128,2,1536]{0,2,1:T(8,128)(2,1)S(1)} all-to-all(bf16[128,2,1536]{0,2,1:T(8,128)(2,1)S(1)} %bitcast.126), channel_id=1, replica_groups=mesh['seq'=2,'tensor'=4,'bucket'=4] {'seq'}, dimensions={1} | all-to-all | bytes 1572864 | tf_op jit(solution)/shard_map/all_to_all | solution.py:18
  39.0 22.6 %all-gather.9.cloned.1.call-done = bf16[384,3072]{1,0:T(8,128)(2,1)} async-done(((bf16[384,768]{1,0:T(8,128)(2,1)}), bf16[384,3072]{1,0:T(8,128)(2,1)}) %all-gather.9.cloned.1.call-update) | async-done | bytes 2359312 | tf_op jit(solution)/shard_map/all_gather | solution.py:69
  62.8 3.5 %all-to-all-start.1 = ((bf16[128,2,1536]{0,2,1:T(8,128)(2,1)}), bf16[128,2,1536]{0,2,1:T(8,128)(2,1)S(1)}, u32[]{:S(2)}, u32[]{:S(2)}) async-start(bf16[128,2,1536]{0,2,1:T(8,128)(2,1)} %bitcast.5), calls=%async_computation.1 | async-start | bytes 1572864 | tf_op jit(solution)/shard_map/all_to_all | solution.py:16
  67.1 10.2 %all-to-all-done.1 = bf16[128,2,1536]{0,2,1:T(8,128)(2,1)S(1)} async-done(((bf16[128,2,1536]{0,2,1:T(8,128)(2,1)}), bf16[128,2,1536]{0,2,1:T(8,128)(2,1)S(1)}, u32[]{:S(2)}, u32[]{:S(2)}) %all-to-all-start.1) | async-done | bytes 786464 | tf_op jit(solution)/shard_map/all_to_all | solution.py:16
  77.3 6.7 %copy.72 = bf16[2,128,1536]{1,0,2:T(2,128)(2,1)S(1)} copy(bf16[2,128,1536]{1,2,0:T(8,128)(2,1)S(1)} %bitcast.122) | data formatting | bytes 1572864 | tf_op jit(solution)/shard_map/all_to_all | solution.py:16
  84.4 41.0 %all-gather.5.cloned.1.call-done = bf16[1024,1536]{1,0:T(8,128)(2,1)} async-done(((bf16[256,1536]{1,0:T(8,128)(2,1)}), bf16[1024,1536]{1,0:T(8,128)(2,1)}) %all-gather.5.cloned.1.call-update) | async-done | bytes 3145744 | tf_op jit(solution)/shard_map/all_gather | solution.py:38
  125.4 2.9 fusion.89
  128.4 1.2 copy.70
  130.1 1.4 copy.80
  131.5 57.6 %all-gather.7.cloned.1.call-done = bf16[1024,1536]{1,0:T(8,128)(2,1)} async-done(((bf16[256,1536]{1,0:T(8,128)(2,1)}), bf16[1024,1536]{1,0:T(8,128)(2,1)}) %all-gather.7.cloned.1.call-update) | async-done | bytes 3145744 | tf_op jit(solution)/shard_map/all_gather | solution.py:39
  189.1 3.6 %fusion.88 = (bf16[256,1536]{1,0:T(8,128)(2,1)}, bf16[256,1536]{1,0:T(8,128)(2,1)}, bf16[256,1536]{1,0:T(8,128)(2,1)}, bf16[256,1536]{1,0:T(8,128)(2,1)}) fusion(bf16[1024,1536]{1,0:T(8,128)(2,1)} %all-gather.7.cloned.1.call-done), kind=kLoop, calls=%fused_computation.155 | loop fusion | bytes 6291456 | tf_op jit(solution)/shard_map/slice | solution.py:45
  192.7 2.3 copy.83
  195.0 2.5 copy.89
  197.5 2.4 copy.95
  199.9 2.5 copy.77
  202.4 1.9 bitcast_reduce_fusion.3
  211.6 1.4 fusion.19
  212.9 1.2 fusion.17
  214.2 3.0 fusion.25
  218.6 16.7 %all_to_all.72 = bf16[2,128,1536]{1,2,0:T(8,128)(2,1)S(1)} all-to-all(bf16[2,128,1536]{1,2,0:T(8,128)(2,1)S(1)} %copy.99), channel_id=1, replica_groups=mesh['seq'=2,'tensor'=4,'bucket'=4] {'seq'}, dimensions={0} | all-to-all | bytes 1572864 | tf_op jit(solution)/shard_map/all_to_all | solution.py:68
  235.3 58.3 %all-gather.11.cloned.1.call-done = bf16[3072,3072]{1,0:T(8,128)(2,1)} async-done(((bf16[384,3072]{1,0:T(8,128)(2,1)}), bf16[3072,3072]{1,0:T(8,128)(2,1)}) %all-gather.11.cloned.1.call-update) | async-done | bytes 18874384 | tf_op jit(solution)/shard_map/all_gather | solution.py:72
  293.5 9.9 %fusion = bf16[1,128,3072]{2,1,0:T(8,128)(2,1)} fusion(bf16[128,3072]{0,1:T(8,128)(2,1)S(1)} %bitcast.115, bf16[3072,3072]{1,0:T(8,128)(2,1)} %all-gather.11.cloned.1.call-done), kind=kOutput, calls=%fused_computation.1 | convolution fusion | flops 2416312320 | bytes 20447232 | tf_op jit(solution)/shard_map/dot_general | solution.py:70
  (44 shorter events, 14.3 us)
Async XLA Ops:
  6.5 18.3 %copy-start = (bf16[1,128,3072]{2,1,0:T(8,128)(2,1)S(1)}, bf16[1,128,3072]{2,1,0:T(8,128)(2,1)}, u32[]{:S(2)}) copy-start(bf16[1,128,3072]{2,1,0:T(8,128)(2,1)} %param.7) | copy-start | bytes 2359300
  6.5 55.1 %all-gather.9.cloned.1.call-start = ((), (), s32[]{:S(2)}) async-start(), calls=%async_computation.6 | async-start | bytes 2949120 | tf_op jit(solution)/shard_map/all_gather | solution.py:69
  7.3 118.2 %all-gather.5.cloned.1.call-start = ((), (), s32[]{:S(2)}) async-start(), calls=%async_computation.4 | async-start | bytes 3932160 | tf_op jit(solution)/shard_map/all_gather | solution.py:38
  24.8 164.3 %all-gather.7.cloned.1.call-start = ((), (), s32[]{:S(2)}) async-start(), calls=%async_computation.5 | async-start | bytes 3932160 | tf_op jit(solution)/shard_map/all_gather | solution.py:39
  25.3 36.4 %copy-start.1 = (bf16[1,128,3072]{2,1,0:T(8,128)(2,1)S(1)}, bf16[1,128,3072]{2,1,0:T(8,128)(2,1)}, u32[]{:S(2)}) copy-start(bf16[1,128,3072]{2,1,0:T(8,128)(2,1)} %param.5) | copy-start | bytes 2359300
  39.0 254.6 %all-gather.11.cloned.1.call-start = ((), (), s32[]{:S(2)}) async-start(), calls=%async_computation.7 | async-start | bytes 21233664 | tf_op jit(solution)/shard_map/all_gather | solution.py:72
  62.8 14.4 %all-to-all-start.1 = ((bf16[128,2,1536]{0,2,1:T(8,128)(2,1)}), bf16[128,2,1536]{0,2,1:T(8,128)(2,1)S(1)}, u32[]{:S(2)}, u32[]{:S(2)}) async-start(bf16[128,2,1536]{0,2,1:T(8,128)(2,1)} %bitcast.5), calls=%async_computation.1 | async-start | bytes 1572864 | tf_op jit(solution)/shard_map/all_to_all | solution.py:16
  208.6 1.7 copy-start.5
  210.4 1.2 copy-start.4
  211.6 1.4 copy-start.3
  212.9 1.2 copy-start.2
Sparse Core Ops, SparseCore 0:
  8.9 52.6 all-gather.8
  63.2 62.1 all-gather.4
  127.0 62.0 all-gather.6
  190.9 102.6 all-gather.10
where the time goes:
time: 311 us; the launch traced here: 310 us
  waiting for transfers between devices  190 us (61%)
  blocking collectives  44 us (14%)
  local copies, waits for them, and re-layouts  32.5 us (10%)
  matrix products  21.1 us (7%)
  between operations  14.1 us (5%)
  other arithmetic  4.22 us (1%)
  starting transfers between devices  3.66 us (1%)
    all_gather x1, waiting for transfers between devices, shards(): lax.all_gather(wide_weight, ('seq', 'bucket'), axis=0, tiled=True)  58.3 us
    all_gather x1, waiting for transfers between devices, shards(): value_rows = lax.all_gather(local_v, 'tensor', axis=0, tiled=True)  57.6 us
    all_gather x1, waiting for transfers between devices, shards(): key_rows = lax.all_gather(local_k, 'tensor', axis=0, tiled=True)  41 us
    all_gather x1, waiting for transfers between devices, shards(): wide_weight = lax.all_gather(out_weight, 'tensor', axis=1, tiled=True)  22.6 us
    all_to_all x1, blocking collectives, shards(): lax.all_to_all(mixed, 'seq', split_axis=0, concat_axis=1, tiled=True)  16.7 us
    all_to_all x1, blocking collectives, shards(): lax.all_to_all(keys[0], 'seq', split_axis=1, concat_axis=0, tiled=True)  14.8 us
    slice x5, local copies, waits for them, and re-layouts, shards(): value_rows[offset * row_count:(offset + 1) * row_count]  13.3 us
    all_to_all x1, blocking collectives, shards(): lax.all_to_all(values[0], 'seq', split_axis=1, concat_axis=0, tiled=True)  12.5 us
  transfers between devices with their start and end apart: 5, of which 5 were waited for; matrix products, arithmetic and copies ran while one was open for 15% of the time, Pallas kernels for 0%

commit v1 on v0

--- a/solution.py
+++ b/solution.py
@@ -5,6 +5,20 @@
 
 HS = 128
 MASKED_SCORE = -1e30
+
+
+def _attach_series_all(view):
+    n_all = lax.axis_size("tensor")
+    u_next = [None] * n_all
+    steps_seen = list(map(lambda i0: (i0, (i0 + 1) % n_all), range(n_all)))
+    u_next[n_all - 1] = view
+    for at in range(n_all - 2, -1, -1):
+        u_next[at] = lax.ppermute(u_next[at + 1], "tensor", steps_seen)
+    main = jnp.concatenate(u_next, axis=0)
+    response = lax.axis_index("tensor")
+    x_now = (response + 1) * view.shape[0]
+    raw_out = jnp.roll(main, x_now, axis=0)
+    return raw_out
 
 
 def shards(queries, keys, values, lengths, out_weight):
@@ -36,7 +50,7 @@
     carried = initial
     first_row = jnp.int32(0)
     key_rows = lax.all_gather(local_k, "tensor", axis=0, tiled=True)
-    value_rows = lax.all_gather(local_v, "tensor", axis=0, tiled=True)
+    value_rows = _attach_series_all(local_v)
     for offset in range(key_rows.shape[0] // row_count):
         row_peak, row_sum, accumulated = carried
         key_tile = key_rows[offset * row_count : (offset + 1) * row_count].reshape(

time: 311 us -> 285 us (0.916)
  waiting for transfers between devices: 190 us -> 153 us
  starting transfers between devices: 3.66 us -> 16.4 us
  blocking collectives: 44 us -> 50.6 us
  local copies, waits for them, and re-layouts: 32.5 us -> 28.1 us
    ppermute x0 -> x3, waiting for transfers between devices: none -> 70.4 us  [_attach_series_all(): u_next[at] = lax.ppermute(u_next[at + 1], 'tensor', steps_seen)]
    all_gather x1 -> x0, waiting for transfers between devices: 57.6 us -> none  [shards(): value_rows = lax.all_gather(local_v, 'tensor', axis=0, tiled=True)]
    all_gather x1, waiting for transfers between devices: 41 us -> 0.01 us  [shards(): key_rows = lax.all_gather(local_k, 'tensor', axis=0, tiled=True)]
    all_gather x1, waiting for transfers between devices: 58.3 us -> 25.5 us  [shards(): lax.all_gather(wide_weight, ('seq', 'bucket'), axis=0, tiled=True)]
    all_gather x1, waiting for transfers between devices: 22.6 us -> 36.6 us  [shards(): wide_weight = lax.all_gather(out_weight, 'tensor', axis=1, tiled=True)]
    ppermute x0 -> x3, starting transfers between devices: none -> 12.7 us  [_attach_series_all(): u_next[at] = lax.ppermute(u_next[at + 1], 'tensor', steps_seen)]
    slice x5 -> x1, local copies, waits for them, and re-layouts: 13.3 us -> 1.85 us  [shards(): value_rows[offset * row_count:(offset + 1) * row_count]]
    all_to_all x1, waiting for transfers between devices: 10.2 us -> 19.4 us  [shards(): lax.all_to_all(queries[0], 'seq', split_axis=1, concat_axis=0, tiled=True)]
  transfers between devices with their start and end apart: 5 -> 7, of which waited for: 5 -> 5; matrix products, arithmetic and copies ran while one was open for 15% -> 14% of each run, Pallas kernels for 0% -> 0%
where the time goes in v1:
time: 285 us; the launch traced here: 284 us
  waiting for transfers between devices  153 us (54%)
  blocking collectives  50.6 us (18%)
  local copies, waits for them, and re-layouts  28.1 us (10%)
  matrix products  18.9 us (7%)
  starting transfers between devices  16.4 us (6%)
  between operations  14.1 us (5%)
  other arithmetic  3.63 us (1%)
    ppermute x3, waiting for transfers between devices, _attach_series_all(): u_next[at] = lax.ppermute(u_next[at + 1], 'tensor', steps_seen)  70.4 us
    all_gather x1, waiting for transfers between devices, shards(): wide_weight = lax.all_gather(out_weight, 'tensor', axis=1, tiled=True)  36.6 us
    all_gather x1, waiting for transfers between devices, shards(): lax.all_gather(wide_weight, ('seq', 'bucket'), axis=0, tiled=True)  25.5 us
    all_to_all x1, blocking collectives, shards(): lax.all_to_all(mixed, 'seq', split_axis=0, concat_axis=1, tiled=True)  22.3 us
    all_to_all x1, waiting for transfers between devices, shards(): lax.all_to_all(queries[0], 'seq', split_axis=1, concat_axis=0, tiled=True)  19.4 us
    all_to_all x1, blocking collectives, shards(): lax.all_to_all(keys[0], 'seq', split_axis=1, concat_axis=0, tiled=True)  14.9 us
    all_to_all x1, blocking collectives, shards(): lax.all_to_all(values[0], 'seq', split_axis=1, concat_axis=0, tiled=True)  13.3 us
    ppermute x3, starting transfers between devices, _attach_series_all(): u_next[at] = lax.ppermute(u_next[at + 1], 'tensor', steps_seen)  12.7 us
  transfers between devices with their start and end apart: 7, of which 5 were waited for; matrix products, arithmetic and copies ran while one was open for 14% of the time, Pallas kernels for 0%

profile of v1, /device:TPU:0, one launch (start us, length us, event | category | flops | bytes accessed | tf_op | source)
XLA Modules:
  0.0 284.2 jit_solution(3437254395051684471)
XLA Ops:
  7.3 1.5 copy.75
  8.8 14.9 %all_to_all.70 = bf16[128,2,1536]{0,2,1:T(8,128)(2,1)S(1)} all-to-all(bf16[128,2,1536]{0,2,1:T(8,128)(2,1)S(1)} %bitcast.126), channel_id=1, replica_groups=mesh['seq'=2,'tensor'=4,'bucket'=4] {'seq'}, dimensions={1} | all-to-all | bytes 1572864 | tf_op jit(solution)/shard_map/all_to_all | solution.py:31
  23.8 1.2 copy.76
  25.1 36.6 %all-gather.6.cloned.1.call-done = bf16[384,3072]{1,0:T(8,128)(2,1)} async-done(((bf16[384,768]{1,0:T(8,128)(2,1)}), bf16[384,3072]{1,0:T(8,128)(2,1)}) %all-gather.6.cloned.1.call-update) | async-done | bytes 2359312 | tf_op jit(solution)/shard_map/all_gather | solution.py:83
  62.3 13.3 %all_to_all.71 = bf16[128,2,1536]{2,0,1:T(8,128)(2,1)S(1)} all-to-all(bf16[128,2,1536]{2,0,1:T(8,128)(2,1)S(1)} %copy.83), channel_id=1, replica_groups=mesh['seq'=2,'tensor'=4,'bucket'=4] {'seq'}, dimensions={1} | all-to-all | bytes 1572864 | tf_op jit(solution)/shard_map/all_to_all | solution.py:32
  76.0 38.4 %collective-permute-done = bf16[256,1536]{0,1:T(8,128)(2,1)S(1)} collective-permute-done((bf16[256,1536]{0,1:T(8,128)(2,1)S(1)}, bf16[256,1536]{0,1:T(8,128)(2,1)S(1)}, u32[]{:S(2)}, u32[]{:S(2)}) %collective-permute-start) | collective-permute-done | bytes 786464 | tf_op jit(solution)/shard_map/ppermute | solution.py:16
  114.4 12.6 %collective-permute-start.1 = (bf16[256,1536]{0,1:T(8,128)(2,1)S(1)}, bf16[256,1536]{0,1:T(8,128)(2,1)S(1)}, u32[]{:S(2)}, u32[]{:S(2)}) collective-permute-start(bf16[256,1536]{0,1:T(8,128)(2,1)S(1)} %collective-permute-done), channel_id=1, source_target_pairs={{0,4},{4,8},{8,12},{12,0},{1,5},{5,9},{9,13},{13,1},{2,6},{6,10},{... | collective-permute-start | bytes 2359304 | tf_op jit(solution)/shard_map/ppermute | solution.py:16
  127.0 32.0 %collective-permute-done.1 = bf16[256,1536]{0,1:T(8,128)(2,1)S(1)} collective-permute-done((bf16[256,1536]{0,1:T(8,128)(2,1)S(1)}, bf16[256,1536]{0,1:T(8,128)(2,1)S(1)}, u32[]{:S(2)}, u32[]{:S(2)}) %collective-permute-start.1) | collective-permute-done | bytes 786464 | tf_op jit(solution)/shard_map/ppermute | solution.py:16
  159.0 2.4 copy.78
  161.5 3.6 %all-to-all-start.1 = ((bf16[128,2,1536]{0,2,1:T(8,128)(2,1)}), bf16[128,2,1536]{0,2,1:T(8,128)(2,1)S(1)}, u32[]{:S(2)}, u32[]{:S(2)}) async-start(bf16[128,2,1536]{0,2,1:T(8,128)(2,1)} %bitcast.123), calls=%async_computation.1 | async-start | bytes 1572864 | tf_op jit(solution)/shard_map/all_to_all | solution.py:30
  165.8 19.4 %all-to-all-done.1 = bf16[128,2,1536]{0,2,1:T(8,128)(2,1)S(1)} async-done(((bf16[128,2,1536]{0,2,1:T(8,128)(2,1)}), bf16[128,2,1536]{0,2,1:T(8,128)(2,1)S(1)}, u32[]{:S(2)}, u32[]{:S(2)}) %all-to-all-start.1) | async-done | bytes 786464 | tf_op jit(solution)/shard_map/all_to_all | solution.py:30
  185.2 7.2 %copy.79 = bf16[2,128,1536]{1,0,2:T(2,128)(2,1)} copy(bf16[2,128,1536]{1,2,0:T(8,128)(2,1)S(1)} %bitcast.122) | data formatting | bytes 1572864 | tf_op jit(solution)/shard_map/all_to_all | solution.py:30
  192.4 2.6 reshape.424
  195.0 1.2 constant_dynamic-update-slice_fusion.7
  196.6 1.2 constant_dynamic-update-slice_fusion.3
  198.2 1.8 constant_dynamic-slice_fusion.3
  200.0 3.1 %fusion.89 = (bf16[256,1536]{1,0:T(8,128)(2,1)}, bf16[256,1536]{1,0:T(8,128)(2,1)S(1)}, bf16[256,1536]{1,0:T(8,128)(2,1)S(1)}, bf16[256,1536]{1,0:T(8,128)(2,1)S(1)}) fusion(bf16[1024,1536]{1,0:T(8,128)(2,1)} %all-gather.4.cloned.1.call-done), kind=kLoop, calls=%fused_computation.168 | loop fusion | bytes 6291456 | tf_op jit(solution)/shard_map/slice | solution.py:56
  203.1 1.2 copy.92
  204.8 1.6 copy.77
  206.5 2.2 bitcast_reduce_fusion.1
  218.1 1.5 fusion.25
  220.0 22.3 %all_to_all.72 = bf16[2,128,1536]{1,2,0:T(8,128)(2,1)S(1)} all-to-all(bf16[2,128,1536]{1,2,0:T(8,128)(2,1)S(1)} %fusion.29), channel_id=1, replica_groups=mesh['seq'=2,'tensor'=4,'bucket'=4] {'seq'}, dimensions={0} | all-to-all | bytes 1572864 | tf_op jit(solution)/shard_map/all_to_all | solution.py:82
  242.3 25.5 %all-gather.8.cloned.1.call-done = bf16[3072,3072]{1,0:T(8,128)(2,1)} async-done(((bf16[384,3072]{1,0:T(8,128)(2,1)}), bf16[3072,3072]{1,0:T(8,128)(2,1)}) %all-gather.8.cloned.1.call-update) | async-done | bytes 18874384 | tf_op jit(solution)/shard_map/all_gather | solution.py:86
  267.8 9.9 %fusion = bf16[1,128,3072]{2,1,0:T(8,128)(2,1)} fusion(bf16[128,3072]{0,1:T(8,128)(2,1)S(1)} %bitcast.116, bf16[3072,3072]{1,0:T(8,128)(2,1)} %all-gather.8.cloned.1.call-done), kind=kOutput, calls=%fused_computation.1 | convolution fusion | flops 2416312320 | bytes 20447232 | tf_op jit(solution)/shard_map/dot_general | solution.py:84
  (48 shorter events, 12.7 us)
Async XLA Ops:
  6.5 55.1 %all-gather.6.cloned.1.call-start = ((), (), s32[]{:S(2)}) async-start(), calls=%async_computation.5 | async-start | bytes 2949120 | tf_op jit(solution)/shard_map/all_gather | solution.py:83
  7.3 192.8 %all-gather.4.cloned.1.call-start = ((), (), s32[]{:S(2)}) async-start(), calls=%async_computation.4 | async-start | bytes 3932160 | tf_op jit(solution)/shard_map/all_gather | solution.py:52
  8.8 52.9 %copy-start = (bf16[1,128,3072]{2,1,0:T(8,128)(2,1)S(1)}, bf16[1,128,3072]{2,1,0:T(8,128)(2,1)}, u32[]{:S(2)}) copy-start(bf16[1,128,3072]{2,1,0:T(8,128)(2,1)} %param.7) | copy-start | bytes 2359300
  25.0 242.8 %all-gather.8.cloned.1.call-start = ((), (), s32[]{:S(2)}) async-start(), calls=%async_computation.6 | async-start | bytes 21233664 | tf_op jit(solution)/shard_map/all_gather | solution.py:86
  75.9 38.5 %collective-permute-start = (bf16[256,1536]{0,1:T(8,128)(2,1)S(1)}, bf16[256,1536]{0,1:T(8,128)(2,1)S(1)}, u32[]{:S(2)}, u32[]{:S(2)}) collective-permute-start(bf16[256,1536]{0,1:T(8,128)(2,1)S(1)} %copy.84), channel_id=1, source_target_pairs={{0,4},{4,8},{8,12},{12,0},{1,5},{5,9},{9,13},{13,1},{2,6},{6,10},{... | collective-permute-start | bytes 2359304 | tf_op jit(solution)/shard_map/ppermute | solution.py:16
  114.4 44.6 %collective-permute-start.1 = (bf16[256,1536]{0,1:T(8,128)(2,1)S(1)}, bf16[256,1536]{0,1:T(8,128)(2,1)S(1)}, u32[]{:S(2)}, u32[]{:S(2)}) collective-permute-start(bf16[256,1536]{0,1:T(8,128)(2,1)S(1)} %collective-permute-done), channel_id=1, source_target_pairs={{0,4},{4,8},{8,12},{12,0},{1,5},{5,9},{9,13},{13,1},{2,6},{6,10},{... | collective-permute-start | bytes 2359304 | tf_op jit(solution)/shard_map/ppermute | solution.py:16
  159.0 36.0 %collective-permute-start.2 = (bf16[256,1536]{0,1:T(8,128)(2,1)S(1)}, bf16[256,1536]{0,1:T(8,128)(2,1)}, u32[]{:S(2)}, u32[]{:S(2)}) collective-permute-start(bf16[256,1536]{0,1:T(8,128)(2,1)S(1)} %collective-permute-done.1), channel_id=1, source_target_pairs={{0,4},{4,8},{8,12},{12,0},{1,5},{5,9},{9,13},{13,1},{2,6},{6,10},{... | collective-permute-start | bytes 2359304 | tf_op jit(solution)/shard_map/ppermute | solution.py:16
  161.5 23.7 %all-to-all-start.1 = ((bf16[128,2,1536]{0,2,1:T(8,128)(2,1)}), bf16[128,2,1536]{0,2,1:T(8,128)(2,1)S(1)}, u32[]{:S(2)}, u32[]{:S(2)}) async-start(bf16[128,2,1536]{0,2,1:T(8,128)(2,1)} %bitcast.123), calls=%async_computation.1 | async-start | bytes 1572864 | tf_op jit(solution)/shard_map/all_to_all | solution.py:30
  213.0 1.7 copy-start.4
  214.7 1.1 copy-start.3
  215.9 1.1 copy-start.2
  217.0 1.1 copy-start.1
Sparse Core Ops, SparseCore 0:
  8.9 52.6 all-gather.5
  63.2 88.6 all-gather.3
  153.8 113.9 all-gather.7
